TPU v7x, 32 devices: a whole 2x2x4 slice. The times are simulated.
32 devices in a mesh: blk: 16 (over z, x, core), rep: 2 (over y).
Axes of the slice: x: 2, y: 2, z: 4, core: 2. Of those that a mesh axis runs over, the one named last changes fastest.
Arguments:
- particles: bfloat16 [896, 2048], P(('blk', 'rep')), may hold values from -0.0029907227 to 0.0029907227
- scores: bfloat16 [896, 2048], P(('blk', 'rep')), may hold values from -60 to 60, as said below
- spread: float32 [1], replicated, may hold values from 0.00034816 to 0.00069632
Outputs:
- direction: float32 [896, 2048], P(('blk', 'rep'))
Inputs may be any that keep to these rules, and one draw needn't show every extreme that they name: `scores`: scores of the particles' log posterior.
All inputs are finite; a program needn't handle non-finite values.
Results may differ from a plain program's by a relative error of at most 0.0003.
Values may be sent and summed in bfloat16 or wider, within the bound.
A program may use at most 128 MiB of HBM per device.

v0:
```python
import jax
import jax.numpy as jnp
from jax import lax
from jax.sharding import PartitionSpec as P


def kernel_weights(targets, target_norm, source_x, inverse):
    cross_dots = lax.dot_general(
        targets, source_x, (((1,), (1,)), ((), ())), preferred_element_type=jnp.float32
    )
    source_wide = source_x.astype(jnp.float32)
    source_norm = jnp.sum(source_wide * source_wide, axis=1)
    squared = jnp.maximum(target_norm[:, None] + source_norm[None, :] - 2.0 * cross_dots, 0.0)
    return jnp.exp(-squared * inverse)


def shards(particles, scores, spread):
    inverse = 1.0 / spread[0]
    own_count = particles.shape[0]
    population = own_count * lax.axis_size("blk") * lax.axis_size("rep")
    targets = lax.all_gather(particles, "rep", axis=0, tiled=True)
    target_wide = targets.astype(jnp.float32)
    target_norm = jnp.sum(target_wide * target_wide, axis=1)
    stacked = jnp.stack([scores, particles], axis=0)
    source = lax.all_gather(stacked, "blk", axis=1, tiled=True)
    weights = kernel_weights(targets, target_norm, source[1], inverse)
    weights_low = weights.astype(jnp.bfloat16)
    combined_step = jnp.einsum(
        "ij,cjd->cid", weights_low, source, preferred_element_type=jnp.float32
    )
    row_total = jnp.sum(weights, axis=1)
    drive_sum = combined_step[0]
    pull_sum = combined_step[1]
    partial_value = (
        drive_sum + 2.0 * inverse * (target_wide * row_total[:, None] - pull_sum)
    ) / population
    return lax.psum_scatter(partial_value, "rep", scatter_dimension=0, tiled=True)


def solution(mesh):
    return jax.shard_map(
        shards,
        mesh=mesh,
        in_specs=(P(("blk", "rep"), None), P(("blk", "rep"), None), P()),
        out_specs=P(("blk", "rep"), None),
        check_vma=False,
    )
```

profile of v0, /device:TPU:0, one launch (start us, length us, event | category | flops | bytes accessed | tf_op | source)
XLA Modules:
  0.0 90.4 jit_solution(13617939061221818914)
XLA Ops:
  6.5 0.0 all-gather.3.cloned.1.call-start
  6.5 1.0 %pad_maximum_fusion = bf16[2,28,2048]{2,1,0:T(8,128)(2,1)S(1)} fusion(bf16[1,28,2048]{2,1,0:T(8,128)(2,1)} %bitcast.53, bf16[1,28,2048]{2,1,0:T(8,128)(2,1)} %bitcast.55), kind=kLoop, calls=%fused_computation.20 | loop fusion | flops 114688 | bytes 458752 | tf_op jit(solution)/shard_map/stack | solution.py:24
  7.5 0.9 %copy.6 = bf16[2,28,2048]{2,0,1:T(2,128)(2,1)} copy(bf16[2,28,2048]{2,1,0:T(8,128)(2,1)S(1)} %pad_maximum_fusion) | data formatting | bytes 458752 | tf_op jit(solution)/shard_map/stack | solution.py:24
  8.5 0.0 all-gather.3.cloned.1.call-update
  8.5 7.4 %all-gather = bf16[2,28,2048]{2,1,0:T(8,128)(2,1)S(1)} all-gather(bf16[1,28,2048]{2,1,0:T(8,128)(2,1)} %bitcast.54), channel_id=1, replica_groups=mesh['blk'=16,'rep'=2] {'rep'}, dimensions={0}, use_global_device_ids=true | all-gather | bytes 344064 | tf_op jit(solution)/shard_map/all_gather | solution.py:21
  15.9 0.1 reshape.6
  16.7 0.2 fusion.9
  16.8 43.2 %all-gather.3.cloned.1.call-done = bf16[2,448,2048]{2,0,1:T(2,128)(2,1)} async-done(((bf16[2,28,2048]{2,0,1:T(2,128)(2,1)}), bf16[2,448,2048]{2,0,1:T(2,128)(2,1)}) %all-gather.3.cloned.1.call-update) | async-done | bytes 3670032 | tf_op jit(solution)/shard_map/all_gather | solution.py:25
  60.0 3.6 %copy.8 = bf16[2,448,2048]{2,1,0:T(8,128)(2,1)S(1)} copy(bf16[2,448,2048]{2,0,1:T(2,128)(2,1)} %all-gather.3.cloned.1.call-done) | data formatting | bytes 7340032 | tf_op jit(solution)/shard_map/all_gather | solution.py:25
  63.7 0.0 copy-start
  63.7 0.4 multiply_reduce_fusion
  64.1 0.8 fusion.17
  64.9 0.8 copy-done
  65.7 0.0 copy-start.1
  65.7 1.2 %convolution_bitcast_fusion = f32[2,56,2048]{2,1,0:T(8,128)S(1)} fusion(bf16[56,448]{1,0:T(8,128)(2,1)S(1)} %get-tuple-element.6, bf16[2,448,2048]{2,0,1:T(2,128)(2,1)S(1)} %copy-done), kind=kOutput, calls=%fused_computation.1 | convolution fusion | flops 205520896 | bytes 4637696 | tf_op jit(solution)/shard_map/ij,cjd->cid/dot_general | solution.py:28
  67.0 0.2 fusion.13
  67.1 11.4 %fusion = f32[32,2048]{1,0:T(8,128)S(1)} fusion(f32[56,2048]{1,0:T(8,128)S(1)} %fusion.13), kind=kCustom, calls=%all-reduce-scatter | all-reduce-scatter fusion | flops 131073 | bytes 721408
  78.5 2.5 %collective-permute-start = (f32[4,2048]{1,0:T(4,128)S(1)}, f32[4,2048]{1,0:T(4,128)S(1)}, u32[]{:S(2)}, u32[]{:S(2)}) collective-permute-start(f32[4,2048]{1,0:T(4,128)S(1)} %slice.15), channel_id=1, source_target_pairs={{0,1},{2,3},{4,5},{6,7},{8,9},{10,11},{12,13},{14,15},{16,17},{18,... | collective-permute-start | bytes 98312
  81.0 0.0 copy-done.1
  81.0 0.6 dynamic-slice.4
  82.2 0.3 collective-permute-done
  82.6 0.2 concatenate
  82.8 0.7 constant_dynamic-slice_fusion
  (1 shorter events, 0.0 us)
Async XLA Ops:
  6.5 53.5 %all-gather.3.cloned.1.call-start = ((), (), s32[]{:S(2)}) async-start(), calls=%async_computation | async-start | bytes 3899392 | tf_op jit(solution)/shard_map/all_gather | solution.py:25
  63.7 2.0 %copy-start = (bf16[2,448,2048]{2,0,1:T(2,128)(2,1)S(1)}, bf16[2,448,2048]{2,0,1:T(2,128)(2,1)}, u32[]{:S(2)}) copy-start(bf16[2,448,2048]{2,0,1:T(2,128)(2,1)} %all-gather.3.cloned.1.call-done) | copy-start | bytes 11010052
  65.7 15.3 %copy-start.1 = (u32[32]{0:T(128)S(1)}, u32[32]{0:T(128)}, u32[]{:S(2)}) copy-start(u32[32]{0:T(128)} %constant.16) | copy-start | bytes 388
  78.5 4.0 %collective-permute-start = (f32[4,2048]{1,0:T(4,128)S(1)}, f32[4,2048]{1,0:T(4,128)S(1)}, u32[]{:S(2)}, u32[]{:S(2)}) collective-permute-start(f32[4,2048]{1,0:T(4,128)S(1)} %slice.15), channel_id=1, source_target_pairs={{0,1},{2,3},{4,5},{6,7},{8,9},{10,11},{12,13},{14,15},{16,17},{18,... | collective-permute-start | bytes 98312
Sparse Core Ops, SparseCore 0:
  9.6 50.3 all-gather.2
where the time goes:
time: 90.7 us; the launch traced here: 90.4 us
  waiting for transfers between devices  43.6 us (48%)
  blocking collectives  18.8 us (21%)
  between operations  14.8 us (16%)
  local copies, waits for them, and re-layouts  7.03 us (8%)
  starting transfers between devices  2.46 us (3%)
  matrix products  2.01 us (2%)
  other arithmetic  1.75 us (2%)
    all_gather x1, waiting for transfers between devices, shards(): source = lax.all_gather(stacked, 'blk', axis=1, tiled=True)  43.2 us
    unnamed x1, blocking collectives  11.4 us
    all_gather x1, blocking collectives, shards(): targets = lax.all_gather(particles, 'rep', axis=0, tiled=True)  7.42 us
    all_gather x1, local copies, waits for them, and re-layouts, shards(): source = lax.all_gather(stacked, 'blk', axis=1, tiled=True)  3.65 us
    unnamed x9, local copies, waits for them, and re-layouts  2.46 us
    unnamed x1, starting transfers between devices  2.46 us
  transfers between devices with their start and end apart: 2, of which 2 were waited for; matrix products, arithmetic and copies ran while one was open for 1% of the time, Pallas kernels for 0%

commit v1 on v0

--- a/solution.py
+++ b/solution.py
@@ -1,7 +1,283 @@
+import functools
+
 import jax
 import jax.numpy as jnp
 from jax import lax
+from jax.experimental import pallas as pl
+from jax.experimental.pallas import tpu as pltpu
 from jax.sharding import PartitionSpec as P
+
+MESH = pl.DeviceIdType.MESH
+GROUP = 4
+
+
+def kernel(
+    n, x_hbm, s_hbm, spread_ref, out_ref, xbuf, sbuf, xpad, spad, pmine, precv, fsend, frecv,
+    load_sem, ring_send, ring_recv, chip_send, chip_recv, pair_send, pair_recv,
+):
+    rows = x_hbm.shape[0]
+    groups, _, per_group, pad_rows, half = xpad.shape
+    population = rows * 2 * 2 * n
+    bufs, pads = (xbuf, sbuf), (xpad, spad)
+    b = lax.axis_index("blk")
+    rep = lax.axis_index("rep")
+    core = b % 2
+    q = b // 2
+    odd = q % 2
+    r = (q // 2) * (1 - odd) + (n - 1 - q // 2) * odd
+
+    def blk_at(position, which):
+        up = position // (n // 2)
+        chip = (1 - up) * (2 * position) + up * (2 * (n - 1 - position) + 1)
+        return chip * 2 + which
+
+    cw = {"blk": blk_at((r + 1) % n, core)}
+    ccw = {"blk": blk_at((r + n - 1) % n, core)}
+    sibling = {"blk": q * 2 + 1 - core}
+    pair = {"rep": 1 - rep}
+
+    order = [0]
+    for s in range(1, n // 2):
+        order += [s, n - s]
+    order.append(n // 2)
+    place = {o: divmod(k, GROUP) for k, o in enumerate(order)}
+
+    def slot(a, g, j, o):
+        grp, at = place[o]
+        return bufs[a].at[grp, j, g * GROUP + at]
+
+    def sem_at(a, j, o):
+        return (a * 2 + j) * n + o
+
+    mine = pl.multiple_of(rep * half, 128)
+    other = pl.multiple_of((1 - rep) * half, 128)
+
+    loads = []
+    for a, ref in enumerate((x_hbm, s_hbm)):
+        for grp in range(groups):
+            for j in range(2):
+                pads[a][grp, j, :, pad_rows - 16:, :] = jnp.zeros(
+                    (per_group, 16, half), pads[a].dtype
+                )
+        copy = pltpu.make_async_copy(
+            ref.at[:, pl.ds(mine, half)], slot(a, 0, 0, 0), load_sem.at[a]
+        )
+        copy.start()
+        loads.append(copy)
+
+    barrier = pltpu.get_barrier_semaphore()
+    for peer in (cw, ccw, sibling, pair):
+        pl.semaphore_signal(barrier, inc=1, device_id=peer, device_id_type=MESH)
+    pl.semaphore_wait(barrier, 4)
+
+    started = []
+
+    def remote(src, dst, send, recv, peer):
+        copy = pltpu.make_async_remote_copy(
+            src_ref=src, dst_ref=dst, send_sem=send, recv_sem=recv,
+            device_id=peer, device_id_type=MESH,
+        )
+        copy.start()
+        started.append(copy)
+
+    def reach(j, way):
+        return n // 2 - (1 if (j == 0) == (way < 0) else 0)
+
+    def ring(a, j, o, way):
+        to = (o + way) % n
+        at = sem_at(a, j, to)
+        remote(slot(a, 0, j, o), slot(a, 0, j, to), ring_send.at[at],
+               ring_recv.at[at], cw if way > 0 else ccw)
+
+    def chip(a, j, o):
+        at = sem_at(a, j, o)
+        remote(slot(a, 0, j, o), slot(a, 1, j, o), chip_send.at[at],
+               chip_recv.at[at], sibling)
+
+    def landed(dst, sem):
+        pltpu.make_async_copy(dst, dst, sem).wait()
+
+    def to_pair(a, ref):
+        remote(ref.at[:, pl.ds(other, half)], slot(a, 0, 1, 0),
+               pair_send.at[a], pair_recv.at[a], pair)
+
+    def first(a, j):
+        ring(a, j, 0, 1)
+        ring(a, j, 0, -1)
+        chip(a, j, 0)
+
+    def hop(a, s, j):
+        for way in (1, -1):
+            if s <= reach(j, way):
+                o = s if way > 0 else n - s
+                landed(slot(a, 0, j, o), ring_recv.at[sem_at(a, j, o)])
+                if s < reach(j, way):
+                    ring(a, j, o, way)
+                chip(a, j, o)
+
+    def from_sibling(a, grp):
+        for j in range(2):
+            for o in order[grp * GROUP:(grp + 1) * GROUP]:
+                landed(slot(a, 1, j, o), chip_recv.at[sem_at(a, j, o)])
+            for i in range(per_group):
+                pads[a][grp, j, i, :rows] = bufs[a][grp, j, i]
+
+    def block(a, grp, j):
+        return pads[a][grp, j].reshape(per_group * pad_rows, half)
+
+    def targets():
+        return jnp.concatenate([xpad[0, 0, 0], xpad[0, 1, 0]], axis=0)
+
+    def gram(grp):
+        from_sibling(0, grp)
+        t = targets()
+        t_wide = t.astype(jnp.float32)
+        t_norm = jnp.sum(t_wide * t_wide, axis=1, keepdims=True)
+        for j in range(2):
+            source = block(0, grp, j)
+            dots = lax.dot_general(
+                t, source, (((1,), (1,)), ((), ())), preferred_element_type=jnp.float32
+            )
+            folded = jnp.zeros((per_group * pad_rows, 128), jnp.float32)
+            for c in range(0, half, 128):
+                wide = source[:, c:c + 128].astype(jnp.float32)
+                folded = folded + wide * wide
+            s_norm = jnp.sum(folded.T, axis=0, keepdims=True)
+            part = t_norm + s_norm - 2.0 * dots
+            pmine[grp, 0, j] = part[:pad_rows]
+            pmine[grp, 1, j] = part[pad_rows:]
+        remote(pmine.at[grp], precv.at[grp], pair_send.at[3 + grp],
+               pair_recv.at[3 + grp], pair)
+
+    to_pair(0, x_hbm)
+    to_pair(1, s_hbm)
+    loads[0].wait()
+    first(0, 0)
+    loads[1].wait()
+    first(1, 0)
+    landed(slot(0, 0, 1, 0), pair_recv.at[0])
+    first(0, 1)
+    done = 0
+    for s in range(1, n // 2 + 1):
+        hop(0, s, 0)
+        hop(0, s, 1)
+        if s == 1:
+            landed(slot(1, 0, 1, 0), pair_recv.at[1])
+            first(1, 1)
+        have = 1 + 2 * s if s < n // 2 else n
+        if s < n // 2:
+            while (done + 1) * GROUP <= have:
+                gram(done)
+                done += 1
+    hop(1, 1, 0)
+    hop(1, 1, 1)
+    while done < groups:
+        gram(done)
+        done += 1
+
+    inverse = 1.0 / jnp.full((1, 1), spread_ref[0], jnp.float32)
+    lane = lax.broadcasted_iota(jnp.int32, (1, per_group * pad_rows), 1)
+    real = (lane % pad_rows) < rows
+
+    def weights(grp, j, jr):
+        total = pmine[grp, jr, j] + precv[grp, 1 - jr, 1 - j]
+        return jnp.exp(-jnp.maximum(total, 0.0) * inverse)
+
+    hop(1, 2, 0)
+    hop(1, 2, 1)
+    row_total = jnp.zeros((2 * pad_rows, 1), jnp.float32)
+    pull = jnp.zeros((2 * pad_rows, half), jnp.float32)
+    kern = []
+    for grp in range(groups):
+        landed(precv.at[grp], pair_recv.at[3 + grp])
+        for j in range(2):
+            w = jnp.concatenate([weights(grp, j, 0), weights(grp, j, 1)], axis=0)
+            row_total = row_total + jnp.sum(
+                jnp.where(real, w, 0.0), axis=1, keepdims=True
+            )
+            low = w.astype(jnp.bfloat16)
+            kern.append(low)
+            pull = pull + jnp.dot(
+                low, block(0, grp, j), preferred_element_type=jnp.float32
+            )
+    base = 2.0 * inverse * (targets().astype(jnp.float32) * row_total - pull)
+
+    done = 0
+    for s in range(3, n // 2 + 1):
+        hop(1, s, 0)
+        hop(1, s, 1)
+        have = 1 + 2 * s if s < n // 2 else n
+        if s < n // 2:
+            while (done + 1) * GROUP <= have:
+                from_sibling(1, done)
+                for j in range(2):
+                    base = base + jnp.dot(
+                        kern[2 * done + j], block(1, done, j),
+                        preferred_element_type=jnp.float32,
+                    )
+                done += 1
+    for grp in range(done, groups):
+        from_sibling(1, grp)
+
+    def finish(jr):
+        value = base[jr * pad_rows:(jr + 1) * pad_rows]
+        for grp in range(done, groups):
+            for j in range(2):
+                value = value + jnp.dot(
+                    kern[2 * grp + j][jr * pad_rows:(jr + 1) * pad_rows],
+                    block(1, grp, j), preferred_element_type=jnp.float32,
+                )
+        return value / population
+
+    fsend[...] = finish(1)
+    remote(fsend, frecv, pair_send.at[2], pair_recv.at[2], pair)
+    out_ref[:, pl.ds(mine, half)] = finish(0)[:rows]
+    landed(frecv, pair_recv.at[2])
+    out_ref[:, pl.ds(other, half)] = frecv[:rows]
+    for copy in started:
+        copy.wait_send()
+
+
+def shards(n, particles, scores, spread):
+    rows, width = particles.shape
+    half = width // 2
+    pad_rows = -(-rows // 16) * 16
+    groups = n // GROUP
+    store = (groups, 2, 2 * GROUP, rows, half)
+    padded = (groups, 2, 2 * GROUP, pad_rows, half)
+    sums = (groups, 2, 2, pad_rows, 2 * GROUP * pad_rows)
+    count = 4 * n
+    return pl.pallas_call(
+        functools.partial(kernel, n),
+        out_shape=jax.ShapeDtypeStruct((rows, width), jnp.float32),
+        in_specs=[
+            pl.BlockSpec(memory_space=pl.ANY),
+            pl.BlockSpec(memory_space=pl.ANY),
+            pl.BlockSpec(memory_space=pltpu.SMEM),
+        ],
+        out_specs=pl.BlockSpec(memory_space=pltpu.VMEM),
+        scratch_shapes=[
+            pltpu.VMEM(store, particles.dtype),
+            pltpu.VMEM(store, scores.dtype),
+            pltpu.VMEM(padded, particles.dtype),
+            pltpu.VMEM(padded, scores.dtype),
+            pltpu.VMEM(sums, jnp.float32),
+            pltpu.VMEM(sums, jnp.float32),
+            pltpu.VMEM((pad_rows, half), jnp.float32),
+            pltpu.VMEM((pad_rows, half), jnp.float32),
+            pltpu.SemaphoreType.DMA((2,)),
+            pltpu.SemaphoreType.DMA((count,)),
+            pltpu.SemaphoreType.DMA((count,)),
+            pltpu.SemaphoreType.DMA((count,)),
+            pltpu.SemaphoreType.DMA((count,)),
+            pltpu.SemaphoreType.DMA((3 + groups,)),
+            pltpu.SemaphoreType.DMA((3 + groups,)),
+        ],
+        compiler_params=pltpu.CompilerParams(
+            collective_id=0, has_side_effects=True, vmem_limit_bytes=60 * 2**20
+        ),
+        name="svgd",
+    )(particles, scores, spread)
 
 
 def kernel_weights(targets, target_norm, source_x, inverse):
@@ -14,7 +290,7 @@
     return jnp.exp(-squared * inverse)
 
 
-def shards(particles, scores, spread):
+def plain(particles, scores, spread):
     inverse = 1.0 / spread[0]
     own_count = particles.shape[0]
     population = own_count * lax.axis_size("blk") * lax.axis_size("rep")
@@ -38,8 +314,17 @@
 
 
 def solution(mesh):
+    n = mesh.shape["blk"] // 2
+    even = mesh.shape["rep"] == 2 and mesh.shape["blk"] % 2 == 0 and n % GROUP == 0
+
+    def body(particles, scores, spread):
+        need = 24 * mesh.shape["blk"] * particles.size
+        if even and n >= 8 and need <= 48 * 2**20:
+            return shards(n, particles, scores, spread)
+        return plain(particles, scores, spread)
+
     return jax.shard_map(
-        shards,
+        body,
         mesh=mesh,
         in_specs=(P(("blk", "rep"), None), P(("blk", "rep"), None), P()),
         out_specs=P(("blk", "rep"), None),

time: 90.7 us -> 44.3 us (0.49)
  waiting for transfers between devices: 43.6 us -> 0 us
  Pallas kernels: 0 us -> 41.8 us
  blocking collectives: 18.8 us -> 0 us
  between operations: 14.8 us -> 0.66 us
  local copies, waits for them, and re-layouts: 7.03 us -> 1.67 us
  starting transfers between devices: 2.46 us -> 0 us
  matrix products: 2.01 us -> 0 us
  other arithmetic: 1.75 us -> 0 us
    all_gather x1 -> x0, waiting for transfers between devices: 43.2 us -> none  [shards(): source = lax.all_gather(stacked, 'blk', axis=1, tiled=True)]
    pallas_call x0 -> x1, Pallas kernels: none -> 41.8 us  [shards(): pl.pallas_call(functools.partial(kernel, n), out_shape=jax.ShapeDtypeStru...]
    unnamed x1 -> x0, blocking collectives: 11.4 us -> none
    all_gather x1 -> x0, blocking collectives: 7.42 us -> none  [shards(): targets = lax.all_gather(particles, 'rep', axis=0, tiled=True)]
    all_gather x1 -> x0, local copies, waits for them, and re-layouts: 3.65 us -> none  [shards(): source = lax.all_gather(stacked, 'blk', axis=1, tiled=True)]
    unnamed x1 -> x0, starting transfers between devices: 2.46 us -> none
    dot_general x2 -> x0, matrix products: 2.01 us -> none  [the longest x1 1.25 us: shards(): jnp.einsum('ij,cjd->cid', weights_low, source, preferred_element_type=jnp...]
    another operation x1 -> x0, other arithmetic: 1 us -> none  [shards(): stacked = jnp.stack([scores, particles], axis=0)]
  transfers between devices with their start and end apart: 2 -> 0, of which waited for: 2 -> 0; matrix products, arithmetic and copies ran while one was open for 1% -> 0% of each run, Pallas kernels for 0% -> 0%
where the time goes in v1:
time: 44.3 us; the launch traced here: 44.2 us
  Pallas kernels  41.8 us (94%)
  local copies, waits for them, and re-layouts  1.67 us (4%)
  between operations  0.66 us (1%)
    pallas_call x1, Pallas kernels, shards(): pl.pallas_call(functools.partial(kernel, n), out_shape=jax.ShapeDtypeStru...  41.8 us
    unnamed x1, local copies, waits for them, and re-layouts  1.67 us

profile of v1, /device:TPU:0, one launch (start us, length us, event | category | flops | bytes accessed | tf_op | source)
XLA Modules:
  0.0 44.2 jit_solution(11347347420688741743)
XLA Ops:
  0.7 41.8 %svgd.1 = f32[28,2048]{1,0:T(8,128)} custom-call(bf16[28,2048]{1,0:T(8,128)(2,1)} %x_hbm.1, bf16[28,2048]{1,0:T(8,128)(2,1)} %s_hbm.1, f32[1]{0:T(128)S(6)} %copy.5.spread_ref), custom_call_target="tpu_custom_call" | custom-call | tf_op jit(solution)/shard_map/svgd/pallas_call | solution.py:250
  42.5 1.7 %copy.6 = f32[28,2048]{1,0:T(8,128)} copy(f32[28,2048]{1,0:T(8,128)} %svgd.1) | data formatting | bytes 458752
